TPU v7x, 32 devices: a whole 2x2x4 slice. The times are simulated.
32 devices in a mesh: gx: 4 (over y, x), gy: 4 (over z), gz: 2 (over core).
Axes of the slice: x: 2, y: 2, z: 4, core: 2. Of those that a mesh axis runs over, the one named last changes fastest.
Arguments:
- nodal_scalar_values: float32 [3, 32, 32, 4096], P(None, 'gx', 'gy', 'gz'), may hold values from -6 to 6
- geometry: float32 [6, 4, 4, 512], P(None, 'gx', 'gy', 'gz'), may hold values from -1.2 to 4, as said below
Outputs:
- assembled: float32 [3, 32, 32, 4096], P(None, 'gx', 'gy', 'gz')
Inputs may be any that keep to these rules, and one draw needn't show every extreme that they name: `geometry`: G00, G11 and G22 are positive; each off-diagonal factor is at most 0.3 times the root of the product of its two diagonal factors in magnitude.
All inputs are finite; a program needn't handle non-finite values.
Results may differ from a plain program's by a relative error of at most 0.00007.
Values sent between devices are 32-bit elements; how exact they have to be, the bound alone decides.
A program may use at most 64 MiB of HBM per device.

v0:
```python
import functools

import jax
import jax.numpy as jnp
import numpy as np
from jax import lax
from jax.experimental import pallas as pl
from jax.experimental.pallas import tpu as pltpu
from jax.sharding import PartitionSpec as P

interior_points = [
    -0.8717401485096066,
    -0.5917001814331423,
    -0.2092992179024789,
    0.2092992179024789,
    0.5917001814331423,
    0.8717401485096066,
]
MESH = pl.DeviceIdType.MESH
STEP = 256
LANES = 128
X_FIRST = True
LAG = 5


def legendre_seven(point):
    previous = 1.0
    current = point
    for order in range(1, 7):
        following = ((2 * order + 1) * point * current - order * previous) / (order + 1)
        previous = current
        current = following
    return current


def gll_tables():
    degree = 7
    points = [-1.0] + interior_points + [1.0]
    values = [legendre_seven(point) for point in points]
    node_count = degree + 1
    weights = np.array([2.0 / (degree * (degree + 1) * value * value) for value in values])
    derivative = np.zeros((node_count, node_count))
    for row_index in range(node_count):
        for col_index in range(node_count):
            if row_index != col_index:
                derivative[row_index, col_index] = values[row_index] / (
                    values[col_index] * (points[row_index] - points[col_index])
                )
    derivative[0, 0] = -degree * (degree + 1) / 4.0
    derivative[node_count - 1, node_count - 1] = degree * (degree + 1) / 4.0
    return (derivative, weights)


def halves(table):
    table = np.asarray(table, np.float32)
    high = table.astype(jnp.bfloat16)
    low = (table - high.astype(np.float32)).astype(jnp.bfloat16)
    return high, low


def tables():
    derivative, weights = gll_tables()
    eye = np.eye(8)
    plane_weight = np.kron(weights, weights)
    forward_xy = np.concatenate([np.kron(derivative, eye), np.kron(eye, derivative)], axis=0)
    back_xy = np.concatenate([np.kron(derivative.T, eye), np.kron(eye, derivative.T)], axis=1)
    back_xy = back_xy * np.tile(plane_weight, 2)[None, :]
    forward_z = np.kron(np.eye(16), derivative.T)
    back_z = np.kron(np.eye(16), derivative)
    high, low = halves(forward_xy)
    forward_xy = np.concatenate([high, high, low, low], axis=1)
    high, low = halves(back_xy)
    back_xy = np.concatenate(
        [np.concatenate([high, high], axis=1), np.concatenate([low, low], axis=1)], axis=0
    )
    high, low = halves(forward_z)
    forward_z = np.tile(np.concatenate([high, low], axis=1), (2, 1))
    high, low = halves(back_z)
    back_z = np.tile(np.concatenate([high, low], axis=1), (2, 1))
    matrices = np.concatenate([forward_xy, back_xy, forward_z, back_z], axis=0)
    plane = np.repeat(plane_weight[:, None], LANES, axis=1)
    along = np.repeat(np.tile(weights, LANES // 8)[None, :], 8, axis=0)
    scales = np.concatenate([plane, along], axis=0).astype(np.float32)
    return matrices, scales


def seat(comp, m):
    if m in (0, 7):
        return 0, 2 * comp + (1 if m == 7 else 0)
    if comp:
        return comp, m - 1
    return (m - 1) // 2, 6 + (m - 1) % 2


def split(value):
    high = value.astype(jnp.bfloat16)
    low = (value - high.astype(jnp.float32)).astype(jnp.bfloat16)
    return high, low


def product(left, right):
    return jnp.dot(left, right, preferred_element_type=jnp.float32)


def along_lanes(pairs, table):
    rows, width = pairs[0][0].shape
    spans = [slice(start, start + LANES) for start in range(0, width, LANES)]
    stacked = [
        jnp.concatenate([high[:, span], low[:, span]], axis=1)
        for high, low in pairs
        for span in spans
    ]
    twice = product(jnp.concatenate(stacked, axis=0), table)
    once = twice[:, :LANES] + twice[:, LANES:]
    pieces = [once[at * rows : (at + 1) * rows] for at in range(len(stacked))]
    return [
        jnp.concatenate(pieces[at : at + len(spans)], axis=1)
        for at in range(0, len(pieces), len(spans))
    ]


def kernel(
    sizes,
    chunk,
    u_hbm,
    geo_hbm,
    mat_hbm,
    scale_hbm,
    out,
    u,
    geo,
    mat,
    scale,
    metric,
    local,
    x_out,
    y_out,
    x_in,
    y_in,
    corner_out,
    corner_in,
    z_out,
    z_in,
    relay,
    in_sem,
    const_sem,
    x_send,
    x_recv,
    y_send,
    y_recv,
    c_send,
    c_recv,
    z_send,
    z_recv,
    r_send,
    r_recv,
    b_send,
    b_recv,
):
    comps, _, _, total = u.shape
    count = total // chunk
    order = [0] + ([count - 1] if count > 1 else []) + list(range(1, count - 1))
    names = ("gx", "gy", "gz")
    place = {name: lax.axis_index(name) for name in names}
    below = {name: place[name] > 0 for name in names}
    above = {name: place[name] < sizes[name] - 1 for name in names}

    const_copies = [
        pltpu.make_async_copy(mat_hbm, mat, const_sem.at[0]),
        pltpu.make_async_copy(scale_hbm, scale, const_sem.at[1]),
        pltpu.make_async_copy(geo_hbm, geo, const_sem.at[2]),
    ]
    for copy in const_copies:
        copy.start()
    in_copies = {}
    for c in order:
        span = pl.ds(c * chunk, chunk)
        in_copies[c] = pltpu.make_async_copy(
            u_hbm.at[:, :, :, span], u.at[:, :, :, span], in_sem.at[c]
        )
        in_copies[c].start()

    barrier = pltpu.get_barrier_semaphore()
    for name in names:
        for there, by in ((below[name], -1), (above[name], 1)):

            @pl.when(there)
            def _(name=name, by=by):
                pl.semaphore_signal(
                    barrier, inc=1, device_id={name: place[name] + by}, device_id_type=MESH
                )

    detour = sizes["gx"] == 4
    relayed = order[: count * 3 // 4] if detour else []
    opposite = lax.rem(place["gx"] + 2, 4)
    if detour:
        pl.semaphore_signal(barrier, inc=1, device_id={"gx": opposite}, device_id_type=MESH)

    for side in range(2):
        there = below if side == 0 else above

        @pl.when(jnp.logical_not(there["gx"]))
        def _(side=side):
            x_in[side] = jnp.zeros(x_in.shape[1:], jnp.float32)

        @pl.when(jnp.logical_not(there["gy"]))
        def _(side=side):
            y_in[side] = jnp.zeros(y_in.shape[1:], jnp.float32)
            corner_in[side] = jnp.zeros(corner_in.shape[1:], jnp.float32)

        @pl.when(jnp.logical_not(there["gz"]))
        def _(side=side):
            z_in[side] = jnp.zeros(z_in.shape[1:], jnp.float32)

    for copy in const_copies:
        copy.wait()

    rows = jnp.concatenate(
        [geo[k, 0] for k in range(6)] + [jnp.zeros((2, geo.shape[-1]), jnp.float32)], axis=0
    )
    lane = lax.broadcasted_iota(jnp.int32, (8, LANES), 1)
    for tile in range(total // LANES):
        first = tile * (LANES // 8)
        block = rows[:, first // LANES * LANES : first // LANES * LANES + LANES]
        spread = jnp.take_along_axis(block, lane // 8 + first % LANES, axis=1)
        metric[:, tile * LANES : (tile + 1) * LANES] = spread * scale[64:72, :]

    def x_copy(side, c):
        span = pl.ds(c * chunk, chunk)
        return pltpu.make_async_remote_copy(
            x_out.at[side, 0, :, span],
            x_in.at[side, 0, :, span],
            x_send.at[side, c],
            x_recv.at[side, c],
            device_id={"gx": place["gx"] + (1 if side == 0 else -1)},
            device_id_type=MESH,
        )

    def bulk_copy(side, c):
        span = pl.ds(c * chunk, chunk)
        return pltpu.make_async_remote_copy(
            x_out.at[side, 1:, :, span],
            x_in.at[side, 1:, :, span],
            b_send.at[side, c],
            b_recv.at[side, c],
            device_id={"gx": place["gx"] + (1 if side == 0 else -1)},
            device_id_type=MESH,
        )

    def middle(side):
        return place["gx"] == 1 + side

    def by_way_of(side):
        return 3 * (1 - side) if X_FIRST else 3 * side

    def hop_copy(side, c):
        span = pl.ds(c * chunk, chunk)
        return pltpu.make_async_remote_copy(
            x_out.at[side, 1:, :, span],
            relay.at[:, :, span],
            b_send.at[side, c],
            r_recv.at[c],
            device_id={"gx": by_way_of(side)},
            device_id_type=MESH,
        )

    def onward_copy(side, c):
        span = pl.ds(c * chunk, chunk)
        return pltpu.make_async_remote_copy(
            relay.at[:, :, span],
            x_in.at[side, 1:, :, span],
            r_send.at[c],
            b_recv.at[side, c],
            device_id={"gx": 2 - side},
            device_id_type=MESH,
        )

    def forward(c):
        for side in range(2):

            @pl.when(place["gx"] == by_way_of(side))
            def _(side=side):
                hop_copy(side, c).wait_recv()
                onward_copy(side, c).start()

    def send_bulk(c):
        for side in range(2):
            if c in relayed:
                straight = jnp.logical_and(target("gx", side), jnp.logical_not(middle(side)))
                when_do(straight, lambda: bulk_copy(side, c).start())
                when_do(middle(side), lambda: hop_copy(side, c).start())
            else:
                when_do(target("gx", side), lambda: bulk_copy(side, c).start())

    def y_copy(side, c):
        span = pl.ds(c * chunk, chunk)
        return pltpu.make_async_remote_copy(
            y_out.at[side, :, :, span],
            y_in.at[side, :, :, span],
            y_send.at[side, c],
            y_recv.at[side, c],
            device_id={"gy": place["gy"] + (1 if side == 0 else -1)},
            device_id_type=MESH,
        )

    def c_copy(side, c):
        span = pl.ds(c * chunk, chunk)
        return pltpu.make_async_remote_copy(
            corner_out.at[side, :, span],
            corner_in.at[side, :, span],
            c_send.at[side, c],
            c_recv.at[side, c],
            device_id={"gy": place["gy"] + (1 if side == 0 else -1)},
            device_id_type=MESH,
        )

    def z_copy(side):
        return pltpu.make_async_remote_copy(
            z_out.at[side],
            z_in.at[side],
            z_send.at[side],
            z_recv.at[side],
            device_id={"gz": place["gz"] + (1 if side == 0 else -1)},
            device_id_type=MESH,
        )

    def target(name, side):
        return above[name] if side == 0 else below[name]

    def source(name, side):
        return below[name] if side == 0 else above[name]

    def when_do(condition, act):
        @pl.when(condition)
        def _():
            act()

    def corners(c):
        lanes = slice(c * chunk, (c + 1) * chunk)
        for side in range(2):
            when_do(source("gx", side), lambda: x_copy(side, c).wait_recv())
        for side in range(2):
            for comp in range(comps):
                for x_side in range(2):
                    at_row = 2 * comp + x_side
                    tile, row = seat(comp, 7 if side == 0 else 0)
                    corner_out[side, at_row : at_row + 1, lanes] = x_in[
                        x_side, tile, row : row + 1, lanes
                    ]
            when_do(target("gy", side), lambda: c_copy(side, c).start())

    forward_xy, back_xy = mat[0:128, :], mat[128:256, :]
    forward_z, back_z = mat[256:512, :], mat[512:768, :]

    greeted = sum(side[name].astype(jnp.int32) for name in names for side in (below, above))
    greeted = greeted + (1 if detour else 0)
    waiting, cornering = list(relayed), list(order)
    for at, c in enumerate(order):
        in_copies[c].wait()
        for start in range(c * chunk, (c + 1) * chunk, STEP):
            lanes = slice(start, start + STEP)
            g00, g11, g22, g01, g02, g12 = [metric[k : k + 1, lanes] for k in range(6)]
            pairs = [split(u[comp, :, :, lanes].reshape(64, STEP)) for comp in range(comps)]
            planes = [
                product(forward_xy, jnp.concatenate([high, low, high, low], axis=0))
                for high, low in pairs
            ]
            grads_z = along_lanes(pairs, forward_z)
            sums, z_pairs = [], []
            for both, grad_z in zip(planes, grads_z):
                grad_x, grad_y = both[:64], both[64:]
                flux_x = g00 * grad_x + g01 * grad_y + g02 * grad_z
                flux_y = g01 * grad_x + g11 * grad_y + g12 * grad_z
                x_high, x_low = split(flux_x)
                y_high, y_low = split(flux_y)
                z_pairs.append(split(g02 * grad_x + g12 * grad_y + g22 * grad_z))
                sums.append(
                    product(back_xy, jnp.concatenate([x_high, y_high, x_low, y_low], axis=0))
                )
            backs_z = along_lanes(z_pairs, back_z)
            weight = jnp.concatenate([scale[0:64, :]] * (STEP // LANES), axis=1)
            for comp in range(comps):
                twice = sums[comp]
                terms = twice[:64] + twice[64:] + weight * backs_z[comp]
                terms = terms.reshape(8, 8, STEP)
                local[comp, :, :, lanes] = terms
                for n in range(8):
                    y_out[0, comp, n : n + 1, lanes] = terms[n, 7:8]
                    y_out[1, comp, n : n + 1, lanes] = terms[n, 0:1]
                    tile, row = seat(comp, n)
                    x_out[0, tile, row : row + 1, lanes] = terms[7, n : n + 1]
                    x_out[1, tile, row : row + 1, lanes] = terms[0, n : n + 1]
        if at == 0:
            pl.semaphore_wait(barrier, greeted)
        for side in range(2):
            when_do(target("gx", side), lambda: x_copy(side, c).start())
            when_do(target("gy", side), lambda: y_copy(side, c).start())
        if at > 2:
            send_bulk(order[at - 3])
        if at >= LAG and cornering:
            corners(cornering.pop(0))
        if at >= LAG + 1 and waiting:
            forward(waiting.pop(0))
    for c in order[-3:]:
        send_bulk(c)
    while waiting or cornering:
        if cornering:
            corners(cornering.pop(0))
        if waiting:
            forward(waiting.pop(0))

    def xy_sum(comp, n, lanes):
        value = local[comp, n, :, lanes]
        from_below = y_in[0, comp, n : n + 1, lanes]
        from_above = y_in[1, comp, n : n + 1, lanes]
        if n in (0, 7):
            x_side = 0 if n == 0 else 1
            at_row = 2 * comp + x_side
            seats = [seat(comp, m) for m in range(8)]
            rows = [x_in[x_side, tile, row : row + 1, lanes] for tile, row in seats]
            value = value + jnp.concatenate(rows, axis=0)
            from_below = from_below + corner_in[0, at_row : at_row + 1, lanes]
            from_above = from_above + corner_in[1, at_row : at_row + 1, lanes]
        where = lax.broadcasted_iota(jnp.int32, value.shape, 0)
        value = value + jnp.where(where == 0, from_below, 0.0)
        return value + jnp.where(where == 7, from_above, 0.0)

    def arrived(c):
        for side in range(2):
            when_do(source("gx", side), lambda: bulk_copy(side, c).wait_recv())
            when_do(source("gy", side), lambda: y_copy(side, c).wait_recv())
            when_do(source("gy", side), lambda: c_copy(side, c).wait_recv())

    def finish(first, last):
        for comp in range(comps):
            for n in range(8):
                value = xy_sum(comp, n, slice(max(first - LANES, 0), min(last + LANES, total)))
                if first == 0:
                    value = jnp.concatenate([z_in[0, comp, n], value], axis=1)
                if last == total:
                    value = jnp.concatenate([value, z_in[1, comp, n]], axis=1)
                width = value.shape[1]
                before = pltpu.roll(value, 1, 1)[:, LANES:-LANES]
                after = pltpu.roll(value, width - 1, 1)[:, LANES:-LANES]
                position = lax.broadcasted_iota(jnp.int32, before.shape, 1) % 8
                extra = jnp.where(position == 7, after, jnp.where(position == 0, before, 0.0))
                out[comp, n, :, first:last] = value[:, LANES:-LANES] + extra

    edge = order[:2] if count > 1 else order
    group = min(2 * chunk, total)
    groups = list(range(total // group))
    here = set()
    z_here = False
    for at, c in enumerate(order):
        arrived(c)
        here.add(c)
        if at == len(edge) - 1:
            for side in range(2):
                lanes = slice(total - LANES, total) if side == 0 else slice(0, LANES)
                for comp in range(comps):
                    for n in range(8):
                        z_out[side, comp, n] = xy_sum(comp, n, lanes)
                when_do(target("gz", side), lambda: z_copy(side).start())
        for g in list(groups):
            first, last = g * group // chunk, (g + 1) * group // chunk
            if all(i in here for i in range(max(first - 1, 0), min(last + 1, count))):
                groups.remove(g)
                ends = g * group, (g + 1) * group
                if not z_here and (ends[0] == 0 or ends[1] == total):
                    z_here = True
                    for side in range(2):
                        when_do(source("gz", side), lambda: z_copy(side).wait_recv())
                finish(*ends)

    for c in order:
        for side in range(2):
            when_do(target("gx", side), lambda: x_copy(side, c).wait_send())
            when_do(target("gx", side), lambda: bulk_copy(side, c).wait_send())
            when_do(target("gy", side), lambda: y_copy(side, c).wait_send())
            when_do(target("gy", side), lambda: c_copy(side, c).wait_send())
    for side in range(2):
        when_do(target("gz", side), lambda: z_copy(side).wait_send())
        for c in relayed:
            when_do(place["gx"] == by_way_of(side), lambda: onward_copy(side, c).wait_send())


def local_part(sizes, nodal_scalar_values, geometry):
    comps, _, _, total = nodal_scalar_values.shape
    chunk = min(256, total)
    count = total // chunk
    matrices, scales = tables()
    f32 = jnp.float32
    dma = pltpu.SemaphoreType.DMA
    any_space = pl.BlockSpec(memory_space=pl.ANY)
    return pl.pallas_call(
        functools.partial(kernel, sizes, chunk),
        out_shape=pltpu.VMEM(nodal_scalar_values.shape, f32),
        in_specs=[any_space] * 4,
        out_specs=pl.BlockSpec(memory_space=pltpu.VMEM),
        scratch_shapes=[
            pltpu.VMEM(nodal_scalar_values.shape, f32),
            pltpu.VMEM(geometry.shape, f32),
            pltpu.VMEM(matrices.shape, jnp.bfloat16),
            pltpu.VMEM(scales.shape, f32),
            pltpu.VMEM((8, total), f32),
            pltpu.VMEM(nodal_scalar_values.shape, f32),
            pltpu.VMEM((2, comps, 8, total), f32),
            pltpu.VMEM((2, comps, 8, total), f32),
            pltpu.VMEM((2, comps, 8, total), f32),
            pltpu.VMEM((2, comps, 8, total), f32),
            pltpu.VMEM((2, 8, total), f32),
            pltpu.VMEM((2, 8, total), f32),
            pltpu.VMEM((2, comps, 8, 8, LANES), f32),
            pltpu.VMEM((2, comps, 8, 8, LANES), f32),
            pltpu.VMEM((comps - 1, 8, total), f32),
            dma((count,)),
            dma((3,)),
            dma((2, count)),
            dma((2, count)),
            dma((2, count)),
            dma((2, count)),
            dma((2, count)),
            dma((2, count)),
            dma((2,)),
            dma((2,)),
            dma((count,)),
            dma((count,)),
            dma((2, count)),
            dma((2, count)),
        ],
        compiler_params=pltpu.CompilerParams(collective_id=0, has_side_effects=True),
        name="poisson",
    )(nodal_scalar_values, geometry, jnp.asarray(matrices), jnp.asarray(scales))


def solution(mesh):
    return jax.shard_map(
        functools.partial(local_part, dict(mesh.shape)),
        mesh=mesh,
        in_specs=(P(None, "gx", "gy", "gz"), P(None, "gx", "gy", "gz")),
        out_specs=P(None, "gx", "gy", "gz"),
        check_vma=False,
    )
```

profile of v0, /device:TPU:0, one launch (start us, length us, event | category | flops | bytes accessed | tf_op | source)
XLA Modules:
  0.0 17.9 jit_solution(15949467979972441722)
XLA Ops:
  0.0 16.8 %poisson.1 = f32[3,8,8,2048]{3,2,1,0:T(8,128)S(1)} custom-call(f32[3,8,8,2048]{3,2,1,0:T(8,128)} %u_hbm.1, f32[6,1,1,256]{3,2,1,0:T(1,128)} %geo_hbm.1, bf16[768,256]{1,0:T(8,128)(2,1)} %constant.4.clone.mat_hbm, f32[72,128]{1,0:T(8,128)} %constant.5.clone.scale_hbm), custom_call_target="tpu_custom_call" | custom-call | tf_op jit(solution)/shard_map/poisson/pallas_call | solution.py:495
  16.8 1.1 %copy.6 = f32[3,8,8,2048]{3,2,1,0:T(8,128)} copy(f32[3,8,8,2048]{3,2,1,0:T(8,128)S(1)} %poisson.1) | data formatting | bytes 3145728
where the time goes:
time: 18 us; the launch traced here: 17.9 us
  Pallas kernels  16.8 us (93%)
  local copies, waits for them, and re-layouts  1.15 us (6%)
    pallas_call x1, Pallas kernels, local_part(): pl.pallas_call(functools.partial(kernel, sizes, chunk), out_shape=pltpu.V...  16.8 us
    unnamed x1, local copies, waits for them, and re-layouts  1.15 us

commit v1 on v0

--- a/solution.py
+++ b/solution.py
@@ -21,6 +21,7 @@
 LANES = 128
 X_FIRST = True
 LAG = 5
+BEHIND = 1
 
 
 def legendre_seven(point):
@@ -119,6 +120,18 @@
     ]
 
 
+def chunk_order(count):
+    return [0] + ([count - 1] if count > 1 else []) + list(range(1, count - 1))
+
+
+def chunk_sets(order):
+    first, rest = order[:2], order[2:]
+    tail = rest[max(len(rest) - 2, 0) :]
+    rest = rest[: max(len(rest) - 2, 0)]
+    pairs = [rest[at : at + 2] for at in range(0, len(rest), 2)]
+    return [[c] for c in first] + pairs + [[c] for c in tail]
+
+
 def kernel(
     sizes,
     chunk,
@@ -137,29 +150,26 @@
     y_out,
     x_in,
     y_in,
-    corner_out,
-    corner_in,
     z_out,
     z_in,
     relay,
     in_sem,
     const_sem,
     x_send,
-    x_recv,
     y_send,
+    z_send,
+    r_send,
+    edge_recv,
+    bulk_recv,
     y_recv,
-    c_send,
-    c_recv,
-    z_send,
     z_recv,
-    r_send,
     r_recv,
-    b_send,
-    b_recv,
 ):
     comps, _, _, total = u.shape
     count = total // chunk
-    order = [0] + ([count - 1] if count > 1 else []) + list(range(1, count - 1))
+    order = chunk_order(count)
+    sets = chunk_sets(order)
+    set_of = {c: at for at, members in enumerate(sets) for c in members}
     names = ("gx", "gy", "gz")
     place = {name: lax.axis_index(name) for name in names}
     below = {name: place[name] > 0 for name in names}
@@ -206,7 +216,6 @@
         @pl.when(jnp.logical_not(there["gy"]))
         def _(side=side):
             y_in[side] = jnp.zeros(y_in.shape[1:], jnp.float32)
-            corner_in[side] = jnp.zeros(corner_in.shape[1:], jnp.float32)
 
         @pl.when(jnp.logical_not(there["gz"]))
         def _(side=side):
@@ -225,26 +234,48 @@
         spread = jnp.take_along_axis(block, lane // 8 + first % LANES, axis=1)
         metric[:, tile * LANES : (tile + 1) * LANES] = spread * scale[64:72, :]
 
-    def x_copy(side, c):
-        span = pl.ds(c * chunk, chunk)
+    def span_of(c):
+        return pl.ds(c * chunk, chunk)
+
+    def beside(name, side):
+        return {name: place[name] + (1 if side == 0 else -1)}
+
+    def remote(source, target, send, recv, device):
         return pltpu.make_async_remote_copy(
-            x_out.at[side, 0, :, span],
-            x_in.at[side, 0, :, span],
-            x_send.at[side, c],
-            x_recv.at[side, c],
-            device_id={"gx": place["gx"] + (1 if side == 0 else -1)},
-            device_id_type=MESH,
+            source, target, send, recv, device_id=device, device_id_type=MESH
+        )
+
+    def edge_copy(side, c):
+        at = (side, 0, slice(None), span_of(c))
+        return remote(
+            x_out.at[at], x_in.at[at], x_send.at[side], edge_recv.at[c], beside("gx", side)
         )
 
     def bulk_copy(side, c):
-        span = pl.ds(c * chunk, chunk)
-        return pltpu.make_async_remote_copy(
-            x_out.at[side, 1:, :, span],
-            x_in.at[side, 1:, :, span],
-            b_send.at[side, c],
-            b_recv.at[side, c],
-            device_id={"gx": place["gx"] + (1 if side == 0 else -1)},
-            device_id_type=MESH,
+        at = (side, slice(1, None), slice(None), span_of(c))
+        return remote(
+            x_out.at[at],
+            x_in.at[at],
+            x_send.at[side],
+            bulk_recv.at[set_of[c]],
+            beside("gx", side),
+        )
+
+    def y_edge_copy(side, c):
+        at = (side, 0, slice(None), span_of(c))
+        return remote(
+            y_out.at[at], y_in.at[at], y_send.at[side], y_recv.at[set_of[c]], beside("gy", side)
+        )
+
+    def y_bulk_copy(side, c):
+        at = (side, slice(1, None), slice(None), span_of(c))
+        return remote(
+            y_out.at[at], y_in.at[at], y_send.at[side], y_recv.at[set_of[c]], beside("gy", side)
+        )
+
+    def z_copy(side):
+        return remote(
+            z_out.at[side], z_in.at[side], z_send.at[side], z_recv.at[side], beside("gz", side)
         )
 
     def middle(side):
@@ -254,26 +285,44 @@
         return 3 * (1 - side) if X_FIRST else 3 * side
 
     def hop_copy(side, c):
-        span = pl.ds(c * chunk, chunk)
-        return pltpu.make_async_remote_copy(
-            x_out.at[side, 1:, :, span],
-            relay.at[:, :, span],
-            b_send.at[side, c],
-            r_recv.at[c],
-            device_id={"gx": by_way_of(side)},
-            device_id_type=MESH,
+        return remote(
+            x_out.at[side, 1:, :, span_of(c)],
+            relay.at[:, :, span_of(c)],
+            x_send.at[side],
+            r_recv.at[relayed.index(c)],
+            {"gx": by_way_of(side)},
         )
 
     def onward_copy(side, c):
-        span = pl.ds(c * chunk, chunk)
-        return pltpu.make_async_remote_copy(
-            relay.at[:, :, span],
-            x_in.at[side, 1:, :, span],
-            r_send.at[c],
-            b_recv.at[side, c],
-            device_id={"gx": 2 - side},
-            device_id_type=MESH,
-        )
+        return remote(
+            relay.at[:, :, span_of(c)],
+            x_in.at[side, 1:, :, span_of(c)],
+            r_send.at[0],
+            bulk_recv.at[set_of[c]],
+            {"gx": 2 - side},
+        )
+
+    def target(name, side):
+        return above[name] if side == 0 else below[name]
+
+    def source(name, side):
+        return below[name] if side == 0 else above[name]
+
+    def when_do(condition, act):
+        @pl.when(condition)
+        def _():
+            act()
+
+    def landed(name, ref, recv):
+        def wait(part):
+            remote(part, part, recv, recv, beside(name, 0)).wait_recv()
+
+        if sizes[name] == 2:
+            wait(ref.at[0])
+        elif sizes[name] > 2:
+            both = jnp.logical_and(below[name], above[name])
+            when_do(both, lambda: wait(ref))
+            when_do(jnp.logical_not(both), lambda: wait(ref.at[0]))
 
     def forward(c):
         for side in range(2):
@@ -292,69 +341,25 @@
             else:
                 when_do(target("gx", side), lambda: bulk_copy(side, c).start())
 
-    def y_copy(side, c):
-        span = pl.ds(c * chunk, chunk)
-        return pltpu.make_async_remote_copy(
-            y_out.at[side, :, :, span],
-            y_in.at[side, :, :, span],
-            y_send.at[side, c],
-            y_recv.at[side, c],
-            device_id={"gy": place["gy"] + (1 if side == 0 else -1)},
-            device_id_type=MESH,
-        )
-
-    def c_copy(side, c):
-        span = pl.ds(c * chunk, chunk)
-        return pltpu.make_async_remote_copy(
-            corner_out.at[side, :, span],
-            corner_in.at[side, :, span],
-            c_send.at[side, c],
-            c_recv.at[side, c],
-            device_id={"gy": place["gy"] + (1 if side == 0 else -1)},
-            device_id_type=MESH,
-        )
-
-    def z_copy(side):
-        return pltpu.make_async_remote_copy(
-            z_out.at[side],
-            z_in.at[side],
-            z_send.at[side],
-            z_recv.at[side],
-            device_id={"gz": place["gz"] + (1 if side == 0 else -1)},
-            device_id_type=MESH,
-        )
-
-    def target(name, side):
-        return above[name] if side == 0 else below[name]
-
-    def source(name, side):
-        return below[name] if side == 0 else above[name]
-
-    def when_do(condition, act):
-        @pl.when(condition)
-        def _():
-            act()
-
-    def corners(c):
+    def y_edges(c):
         lanes = slice(c * chunk, (c + 1) * chunk)
+        landed("gx", x_in.at[:, 0, :, span_of(c)], edge_recv.at[c])
+        low, high = x_in[0, 0, :, lanes], x_in[1, 0, :, lanes]
+        row = lax.broadcasted_iota(jnp.int32, low.shape, 0)
+        even, edge = row % 2 == 0, row < 2 * comps
+        extra = jnp.where(even, pltpu.roll(low, 7, 0), high)
+        y_out[0, 0, :, lanes] = y_out[0, 0, :, lanes] + jnp.where(edge, extra, 0.0)
+        extra = jnp.where(even, low, pltpu.roll(high, 1, 0))
+        y_out[1, 0, :, lanes] = y_out[1, 0, :, lanes] + jnp.where(edge, extra, 0.0)
         for side in range(2):
-            when_do(source("gx", side), lambda: x_copy(side, c).wait_recv())
-        for side in range(2):
-            for comp in range(comps):
-                for x_side in range(2):
-                    at_row = 2 * comp + x_side
-                    tile, row = seat(comp, 7 if side == 0 else 0)
-                    corner_out[side, at_row : at_row + 1, lanes] = x_in[
-                        x_side, tile, row : row + 1, lanes
-                    ]
-            when_do(target("gy", side), lambda: c_copy(side, c).start())
+            when_do(target("gy", side), lambda: y_edge_copy(side, c).start())
 
     forward_xy, back_xy = mat[0:128, :], mat[128:256, :]
     forward_z, back_z = mat[256:512, :], mat[512:768, :]
 
     greeted = sum(side[name].astype(jnp.int32) for name in names for side in (below, above))
     greeted = greeted + (1 if detour else 0)
-    waiting, cornering = list(relayed), list(order)
+    waiting, edging = list(relayed), list(order)
     for at, c in enumerate(order):
         in_copies[c].wait()
         for start in range(c * chunk, (c + 1) * chunk, STEP):
@@ -385,51 +390,49 @@
                 terms = terms.reshape(8, 8, STEP)
                 local[comp, :, :, lanes] = terms
                 for n in range(8):
-                    y_out[0, comp, n : n + 1, lanes] = terms[n, 7:8]
-                    y_out[1, comp, n : n + 1, lanes] = terms[n, 0:1]
                     tile, row = seat(comp, n)
+                    y_out[0, tile, row : row + 1, lanes] = terms[n, 7:8]
+                    y_out[1, tile, row : row + 1, lanes] = terms[n, 0:1]
                     x_out[0, tile, row : row + 1, lanes] = terms[7, n : n + 1]
                     x_out[1, tile, row : row + 1, lanes] = terms[0, n : n + 1]
         if at == 0:
             pl.semaphore_wait(barrier, greeted)
         for side in range(2):
-            when_do(target("gx", side), lambda: x_copy(side, c).start())
-            when_do(target("gy", side), lambda: y_copy(side, c).start())
-        if at > 2:
-            send_bulk(order[at - 3])
-        if at >= LAG and cornering:
-            corners(cornering.pop(0))
+            when_do(target("gx", side), lambda: edge_copy(side, c).start())
+            when_do(target("gy", side), lambda: y_bulk_copy(side, c).start())
+        if at >= BEHIND:
+            send_bulk(order[at - BEHIND])
+        if at >= LAG and edging:
+            y_edges(edging.pop(0))
         if at >= LAG + 1 and waiting:
             forward(waiting.pop(0))
-    for c in order[-3:]:
+    for c in order[count - min(BEHIND, count) :]:
         send_bulk(c)
-    while waiting or cornering:
-        if cornering:
-            corners(cornering.pop(0))
+    while waiting or edging:
+        if edging:
+            y_edges(edging.pop(0))
         if waiting:
             forward(waiting.pop(0))
 
     def xy_sum(comp, n, lanes):
         value = local[comp, n, :, lanes]
-        from_below = y_in[0, comp, n : n + 1, lanes]
-        from_above = y_in[1, comp, n : n + 1, lanes]
+        tile, row = seat(comp, n)
+        from_below = y_in[0, tile, row : row + 1, lanes]
+        from_above = y_in[1, tile, row : row + 1, lanes]
         if n in (0, 7):
             x_side = 0 if n == 0 else 1
-            at_row = 2 * comp + x_side
             seats = [seat(comp, m) for m in range(8)]
             rows = [x_in[x_side, tile, row : row + 1, lanes] for tile, row in seats]
             value = value + jnp.concatenate(rows, axis=0)
-            from_below = from_below + corner_in[0, at_row : at_row + 1, lanes]
-            from_above = from_above + corner_in[1, at_row : at_row + 1, lanes]
         where = lax.broadcasted_iota(jnp.int32, value.shape, 0)
         value = value + jnp.where(where == 0, from_below, 0.0)
         return value + jnp.where(where == 7, from_above, 0.0)
 
-    def arrived(c):
-        for side in range(2):
-            when_do(source("gx", side), lambda: bulk_copy(side, c).wait_recv())
-            when_do(source("gy", side), lambda: y_copy(side, c).wait_recv())
-            when_do(source("gy", side), lambda: c_copy(side, c).wait_recv())
+    def arrived(at):
+        members = sets[at]
+        span = pl.ds(members[0] * chunk, len(members) * chunk)
+        landed("gx", x_in.at[:, 1:, :, span], bulk_recv.at[at])
+        landed("gy", y_in.at[:, :, :, span], y_recv.at[at])
 
     def finish(first, last):
         for comp in range(comps):
@@ -446,52 +449,64 @@
                 extra = jnp.where(position == 7, after, jnp.where(position == 0, before, 0.0))
                 out[comp, n, :, first:last] = value[:, LANES:-LANES] + extra
 
-    edge = order[:2] if count > 1 else order
-    group = min(2 * chunk, total)
-    groups = list(range(total // group))
-    here = set()
-    z_here = False
-    for at, c in enumerate(order):
-        arrived(c)
-        here.add(c)
-        if at == len(edge) - 1:
+    def sent(out_ref, in_ref, send, side):
+        remote(out_ref.at[side], in_ref.at[side], send.at[side], send.at[side], beside("gz", 0)).wait_send()
+
+    def onward_sent():
+        part = relay.at[:, :, pl.ds(0, len(relayed) * chunk)]
+        remote(part, part, r_send.at[0], r_send.at[0], beside("gz", 0)).wait_send()
+
+    tiles = total // LANES
+    todo, here = set(range(tiles)), set()
+    ends_here = False
+    for at, members in enumerate(sets):
+        arrived(at)
+        for c in members:
+            here |= set(range(c * chunk // LANES, (c + 1) * chunk // LANES))
+        if {0, tiles - 1} <= here and not ends_here:
+            ends_here = True
             for side in range(2):
                 lanes = slice(total - LANES, total) if side == 0 else slice(0, LANES)
                 for comp in range(comps):
                     for n in range(8):
                         z_out[side, comp, n] = xy_sum(comp, n, lanes)
                 when_do(target("gz", side), lambda: z_copy(side).start())
-        for g in list(groups):
-            first, last = g * group // chunk, (g + 1) * group // chunk
-            if all(i in here for i in range(max(first - 1, 0), min(last + 1, count))):
-                groups.remove(g)
-                ends = g * group, (g + 1) * group
-                if not z_here and (ends[0] == 0 or ends[1] == total):
-                    z_here = True
-                    for side in range(2):
-                        when_do(source("gz", side), lambda: z_copy(side).wait_recv())
-                finish(*ends)
-
-    for c in order:
-        for side in range(2):
-            when_do(target("gx", side), lambda: x_copy(side, c).wait_send())
-            when_do(target("gx", side), lambda: bulk_copy(side, c).wait_send())
-            when_do(target("gy", side), lambda: y_copy(side, c).wait_send())
-            when_do(target("gy", side), lambda: c_copy(side, c).wait_send())
+            if count > 2:
+                continue
+        if not ends_here:
+            continue
+        if {0, tiles - 1} <= todo:
+            for side in range(2):
+                when_do(source("gz", side), lambda: z_copy(side).wait_recv())
+        ready = sorted(
+            t for t in todo if all(0 > o or o >= tiles or o in here for o in (t - 1, t, t + 1))
+        )
+        todo -= set(ready)
+        while ready:
+            first = last = ready.pop(0)
+            while ready and ready[0] == last + 1:
+                last = ready.pop(0)
+            finish(first * LANES, (last + 1) * LANES)
+
     for side in range(2):
+        when_do(target("gx", side), lambda: sent(x_out, x_in, x_send, side))
+        when_do(target("gy", side), lambda: sent(y_out, y_in, y_send, side))
         when_do(target("gz", side), lambda: z_copy(side).wait_send())
-        for c in relayed:
-            when_do(place["gx"] == by_way_of(side), lambda: onward_copy(side, c).wait_send())
+    if relayed:
+        when_do(jnp.logical_or(place["gx"] == 0, place["gx"] == 3), onward_sent)
 
 
 def local_part(sizes, nodal_scalar_values, geometry):
     comps, _, _, total = nodal_scalar_values.shape
     chunk = min(256, total)
     count = total // chunk
+    sets = len(chunk_sets(chunk_order(count)))
     matrices, scales = tables()
     f32 = jnp.float32
     dma = pltpu.SemaphoreType.DMA
     any_space = pl.BlockSpec(memory_space=pl.ANY)
+    plane = pltpu.VMEM((2, comps, 8, total), f32)
+    column = pltpu.VMEM((2, comps, 8, 8, LANES), f32)
     return pl.pallas_call(
         functools.partial(kernel, sizes, chunk),
         out_shape=pltpu.VMEM(nodal_scalar_values.shape, f32),
@@ -504,29 +519,24 @@
             pltpu.VMEM(scales.shape, f32),
             pltpu.VMEM((8, total), f32),
             pltpu.VMEM(nodal_scalar_values.shape, f32),
-            pltpu.VMEM((2, comps, 8, total), f32),
-            pltpu.VMEM((2, comps, 8, total), f32),
-            pltpu.VMEM((2, comps, 8, total), f32),
-            pltpu.VMEM((2, comps, 8, total), f32),
-            pltpu.VMEM((2, 8, total), f32),
-            pltpu.VMEM((2, 8, total), f32),
-            pltpu.VMEM((2, comps, 8, 8, LANES), f32),
-            pltpu.VMEM((2, comps, 8, 8, LANES), f32),
+            plane,
+            plane,
+            plane,
+            plane,
+            column,
+            column,
             pltpu.VMEM((comps - 1, 8, total), f32),
             dma((count,)),
             dma((3,)),
-            dma((2, count)),
-            dma((2, count)),
-            dma((2, count)),
-            dma((2, count)),
-            dma((2, count)),
-            dma((2, count)),
             dma((2,)),
             dma((2,)),
+            dma((2,)),
+            dma((1,)),
             dma((count,)),
-            dma((count,)),
-            dma((2, count)),
-            dma((2, count)),
+            dma((sets,)),
+            dma((sets,)),
+            dma((2,)),
+            dma((max(count * 3 // 4, 1),)),
         ],
         compiler_params=pltpu.CompilerParams(collective_id=0, has_side_effects=True),
         name="poisson",

time: 18 us -> 16.9 us (0.939)
  Pallas kernels: 16.8 us -> 15.6 us
    pallas_call x1, Pallas kernels: 16.8 us -> 15.6 us  [local_part(): pl.pallas_call(functools.partial(kernel, sizes, chunk), out_shape=pltpu.V...]
where the time goes in v1:
time: 16.9 us; the launch traced here: 16.8 us
  Pallas kernels  15.6 us (92%)
  local copies, waits for them, and re-layouts  1.15 us (7%)
    pallas_call x1, Pallas kernels, local_part(): pl.pallas_call(functools.partial(kernel, sizes, chunk), out_shape=pltpu.V...  15.6 us
    unnamed x1, local copies, waits for them, and re-layouts  1.15 us

profile of v1, /device:TPU:0, one launch (start us, length us, event | category | flops | bytes accessed | tf_op | source)
XLA Modules:
  0.0 16.8 jit_solution(14462241013847348642)
XLA Ops:
  0.0 15.6 %poisson.1 = f32[3,8,8,2048]{3,2,1,0:T(8,128)S(1)} custom-call(f32[3,8,8,2048]{3,2,1,0:T(8,128)} %u_hbm.1, f32[6,1,1,256]{3,2,1,0:T(1,128)} %geo_hbm.1, bf16[768,256]{1,0:T(8,128)(2,1)} %constant.4.clone.mat_hbm, f32[72,128]{1,0:T(8,128)} %constant.5.clone.scale_hbm), custom_call_target="tpu_custom_call" | custom-call | tf_op jit(solution)/shard_map/poisson/pallas_call | solution.py:510
  15.6 1.1 %copy.6 = f32[3,8,8,2048]{3,2,1,0:T(8,128)} copy(f32[3,8,8,2048]{3,2,1,0:T(8,128)S(1)} %poisson.1) | data formatting | bytes 3145728

commit v2 on v1

--- a/solution.py
+++ b/solution.py
@@ -17,11 +17,13 @@
     0.8717401485096066,
 ]
 MESH = pl.DeviceIdType.MESH
-STEP = 256
+STEP = 512
 LANES = 128
 X_FIRST = True
-LAG = 5
-BEHIND = 1
+LAG = 4
+BEHIND = 2
+X_EDGE = 7
+Y_EDGE = (6, 7)
 
 
 def legendre_seven(point):
@@ -85,12 +87,71 @@
     return matrices, scales
 
 
-def seat(comp, m):
-    if m in (0, 7):
-        return 0, 2 * comp + (1 if m == 7 else 0)
+def row_index(shape):
+    return lax.broadcasted_iota(jnp.int32, shape, 0)
+
+
+def pack(planes, edge):
+    first, second, third = planes
+    turn = (row_index(first.shape) + (8 - edge)) % 8
+    own = turn < 2
+    second_edge = jnp.logical_and(turn >= 2, turn < 4)
+    third_edge = jnp.logical_and(turn >= 4, turn < 6)
+    edges = jnp.where(
+        second_edge,
+        pltpu.roll(second, 2, 0),
+        jnp.where(third_edge, pltpu.roll(third, 4, 0), first),
+    )
+    return [
+        edges,
+        jnp.where(own, pltpu.roll(first, 6, 0), second),
+        jnp.where(own, pltpu.roll(first, 4, 0), third),
+    ]
+
+
+def unpack(tiles, comp, edge):
+    turn = (row_index(tiles[0].shape) + (8 - edge)) % 8
     if comp:
-        return comp, m - 1
-    return (m - 1) // 2, 6 + (m - 1) % 2
+        return jnp.where(turn < 2, pltpu.roll(tiles[0], 8 - 2 * comp, 0), tiles[comp])
+    from_second = jnp.logical_and(turn >= 2, turn < 4)
+    from_third = jnp.logical_and(turn >= 4, turn < 6)
+    return jnp.where(
+        from_second,
+        pltpu.roll(tiles[1], 2, 0),
+        jnp.where(from_third, pltpu.roll(tiles[2], 4, 0), tiles[0]),
+    )
+
+
+def y_planes(terms):
+    turn = (row_index(terms[0].shape) + 1) % 8
+
+    def gather(four):
+        return jnp.where(
+            turn < 2,
+            four[0],
+            jnp.where(
+                turn < 4,
+                pltpu.roll(four[1], 2, 0),
+                jnp.where(turn < 6, pltpu.roll(four[2], 4, 0), pltpu.roll(four[3], 6, 0)),
+            ),
+        )
+
+    low, high = gather(terms[:4]), pltpu.roll(gather(terms[4:]), 1, 0)
+    even = turn % 2 == 0
+    return jnp.where(even, low, high), jnp.where(even, high, low)
+
+
+def y_seat(side, comp, n):
+    edge = Y_EDGE[side]
+    row = (2 * n + 7 + side) % 8 if n < 4 else 2 * (n - 4) + side
+    turn = (row - edge) % 8
+    if turn < 2:
+        return 0, (row + 2 * comp) % 8
+    if comp:
+        return comp, row
+    if turn < 6:
+        return turn // 2, (row - 2 * (turn // 2)) % 8
+    return 0, row
 
 
 def split(value):
@@ -344,13 +405,12 @@
     def y_edges(c):
         lanes = slice(c * chunk, (c + 1) * chunk)
         landed("gx", x_in.at[:, 0, :, span_of(c)], edge_recv.at[c])
-        low, high = x_in[0, 0, :, lanes], x_in[1, 0, :, lanes]
-        row = lax.broadcasted_iota(jnp.int32, low.shape, 0)
-        even, edge = row % 2 == 0, row < 2 * comps
-        extra = jnp.where(even, pltpu.roll(low, 7, 0), high)
-        y_out[0, 0, :, lanes] = y_out[0, 0, :, lanes] + jnp.where(edge, extra, 0.0)
-        extra = jnp.where(even, low, pltpu.roll(high, 1, 0))
-        y_out[1, 0, :, lanes] = y_out[1, 0, :, lanes] + jnp.where(edge, extra, 0.0)
+        low, high = x_in[0, 0, :, lanes], pltpu.roll(x_in[1, 0, :, lanes], 7, 0)
+        for side in range(2):
+            turn = (row_index(low.shape) + (8 - Y_EDGE[side])) % 8
+            extra = jnp.where(turn % 2 == 1, low, high)
+            extra = jnp.where(turn < 6, extra, 0.0)
+            y_out[side, 0, :, lanes] = y_out[side, 0, :, lanes] + extra
         for side in range(2):
             when_do(target("gy", side), lambda: y_edge_copy(side, c).start())
 
@@ -384,17 +444,21 @@
                 )
             backs_z = along_lanes(z_pairs, back_z)
             weight = jnp.concatenate([scale[0:64, :]] * (STEP // LANES), axis=1)
+            ends = ([], [])
+            sides = ([], [])
             for comp in range(comps):
                 twice = sums[comp]
                 terms = twice[:64] + twice[64:] + weight * backs_z[comp]
                 terms = terms.reshape(8, 8, STEP)
                 local[comp, :, :, lanes] = terms
-                for n in range(8):
-                    tile, row = seat(comp, n)
-                    y_out[0, tile, row : row + 1, lanes] = terms[n, 7:8]
-                    y_out[1, tile, row : row + 1, lanes] = terms[n, 0:1]
-                    x_out[0, tile, row : row + 1, lanes] = terms[7, n : n + 1]
-                    x_out[1, tile, row : row + 1, lanes] = terms[0, n : n + 1]
+                for side, plane in enumerate(y_planes([terms[n] for n in range(8)])):
+                    sides[side].append(plane)
+                    ends[side].append(terms[7 if side == 0 else 0])
+            for side in range(2):
+                for tile, value in enumerate(pack(ends[side], X_EDGE)):
+                    x_out[side, tile, :, lanes] = value
+                for tile, value in enumerate(pack(sides[side], Y_EDGE[side])):
+                    y_out[side, tile, :, lanes] = value
         if at == 0:
             pl.semaphore_wait(barrier, greeted)
         for side in range(2):
@@ -416,17 +480,16 @@
 
     def xy_sum(comp, n, lanes):
         value = local[comp, n, :, lanes]
-        tile, row = seat(comp, n)
-        from_below = y_in[0, tile, row : row + 1, lanes]
-        from_above = y_in[1, tile, row : row + 1, lanes]
+        rows = []
+        for side in range(2):
+            tile, row = y_seat(side, comp, n)
+            rows.append(y_in[side, tile, row : row + 1, lanes])
         if n in (0, 7):
-            x_side = 0 if n == 0 else 1
-            seats = [seat(comp, m) for m in range(8)]
-            rows = [x_in[x_side, tile, row : row + 1, lanes] for tile, row in seats]
-            value = value + jnp.concatenate(rows, axis=0)
-        where = lax.broadcasted_iota(jnp.int32, value.shape, 0)
-        value = value + jnp.where(where == 0, from_below, 0.0)
-        return value + jnp.where(where == 7, from_above, 0.0)
+            side = 0 if n == 0 else 1
+            tiles = [x_in[side, tile, :, lanes] for tile in range(comps)]
+            value = value + unpack(tiles, comp, X_EDGE)
+        where = row_index(value.shape)
+        return value + jnp.where(where == 0, rows[0], jnp.where(where == 7, rows[1], 0.0))
 
     def arrived(at):
         members = sets[at]
@@ -457,13 +520,14 @@
         remote(part, part, r_send.at[0], r_send.at[0], beside("gz", 0)).wait_send()
 
     tiles = total // LANES
-    todo, here = set(range(tiles)), set()
+    outer = {0, tiles - 1}
+    todo, here = set(range(tiles)) - outer, set()
     ends_here = False
     for at, members in enumerate(sets):
         arrived(at)
         for c in members:
             here |= set(range(c * chunk // LANES, (c + 1) * chunk // LANES))
-        if {0, tiles - 1} <= here and not ends_here:
+        if outer <= here and not ends_here:
             ends_here = True
             for side in range(2):
                 lanes = slice(total - LANES, total) if side == 0 else slice(0, LANES)
@@ -471,22 +535,17 @@
                     for n in range(8):
                         z_out[side, comp, n] = xy_sum(comp, n, lanes)
                 when_do(target("gz", side), lambda: z_copy(side).start())
-            if count > 2:
-                continue
-        if not ends_here:
-            continue
-        if {0, tiles - 1} <= todo:
-            for side in range(2):
-                when_do(source("gz", side), lambda: z_copy(side).wait_recv())
-        ready = sorted(
-            t for t in todo if all(0 > o or o >= tiles or o in here for o in (t - 1, t, t + 1))
-        )
+        ready = sorted(t for t in todo if {t - 1, t, t + 1} <= here)
         todo -= set(ready)
         while ready:
             first = last = ready.pop(0)
             while ready and ready[0] == last + 1:
                 last = ready.pop(0)
             finish(first * LANES, (last + 1) * LANES)
+    for side in range(2):
+        when_do(source("gz", side), lambda: z_copy(side).wait_recv())
+    for t in sorted(outer):
+        finish(t * LANES, (t + 1) * LANES)
 
     for side in range(2):
         when_do(target("gx", side), lambda: sent(x_out, x_in, x_send, side))
@@ -498,7 +557,7 @@
 
 def local_part(sizes, nodal_scalar_values, geometry):
     comps, _, _, total = nodal_scalar_values.shape
-    chunk = min(256, total)
+    chunk = min(STEP, total)
     count = total // chunk
     sets = len(chunk_sets(chunk_order(count)))
     matrices, scales = tables()

time: 16.9 us -> 16 us (0.947)
  Pallas kernels: 15.6 us -> 14.7 us
    pallas_call x1, Pallas kernels: 15.6 us -> 14.7 us  [local_part(): pl.pallas_call(functools.partial(kernel, sizes, chunk), out_shape=pltpu.V...]
where the time goes in v2:
time: 16 us; the launch traced here: 15.8 us
  Pallas kernels  14.7 us (92%)
  local copies, waits for them, and re-layouts  1.15 us (7%)
    pallas_call x1, Pallas kernels, local_part(): pl.pallas_call(functools.partial(kernel, sizes, chunk), out_shape=pltpu.V...  14.7 us
    unnamed x1, local copies, waits for them, and re-layouts  1.15 us

profile of v2, /device:TPU:0, one launch (start us, length us, event | category | flops | bytes accessed | tf_op | source)
XLA Modules:
  0.0 15.8 jit_solution(3602808220438840886)
XLA Ops:
  0.0 14.7 %poisson.1 = f32[3,8,8,2048]{3,2,1,0:T(8,128)S(1)} custom-call(f32[3,8,8,2048]{3,2,1,0:T(8,128)} %u_hbm.1, f32[6,1,1,256]{3,2,1,0:T(1,128)} %geo_hbm.1, bf16[768,256]{1,0:T(8,128)(2,1)} %constant.4.clone.mat_hbm, f32[72,128]{1,0:T(8,128)} %constant.5.clone.scale_hbm), custom_call_target="tpu_custom_call" | custom-call | tf_op jit(solution)/shard_map/poisson/pallas_call | solution.py:569
  14.7 1.1 %copy.6 = f32[3,8,8,2048]{3,2,1,0:T(8,128)} copy(f32[3,8,8,2048]{3,2,1,0:T(8,128)S(1)} %poisson.1) | data formatting | bytes 3145728

commit v3 on v2

--- a/solution.py
+++ b/solution.py
@@ -20,8 +20,11 @@
 STEP = 512
 LANES = 128
 X_FIRST = True
-LAG = 4
-BEHIND = 2
+BEHIND = 1
+EARLY_BULK = 2
+RELAYED = 3
+EDGES_FIRST = 2
+OUTER_EARLY = 0
 X_EDGE = 7
 Y_EDGE = (6, 7)
 
@@ -181,21 +184,31 @@
     ]
 
 
+def chunk_spans(total):
+    if total % STEP or total < 2 * STEP:
+        return [(0, total)]
+    widths = [STEP // 2] + [STEP] * (total // STEP - 1) + [STEP // 2]
+    starts = [sum(widths[:at]) for at in range(len(widths))]
+    return list(zip(starts, widths))
+
+
 def chunk_order(count):
     return [0] + ([count - 1] if count > 1 else []) + list(range(1, count - 1))
 
 
-def chunk_sets(order):
-    first, rest = order[:2], order[2:]
-    tail = rest[max(len(rest) - 2, 0) :]
-    rest = rest[: max(len(rest) - 2, 0)]
-    pairs = [rest[at : at + 2] for at in range(0, len(rest), 2)]
-    return [[c] for c in first] + pairs + [[c] for c in tail]
+def relayed_chunks(spans):
+    total = sum(width for _, width in spans)
+    chosen, lanes = [], 0
+    for c in chunk_order(len(spans)):
+        if (lanes + spans[c][1]) * 4 <= total * RELAYED:
+            chosen.append(c)
+            lanes += spans[c][1]
+    return chosen
 
 
 def kernel(
     sizes,
-    chunk,
+    spans,
     u_hbm,
     geo_hbm,
     mat_hbm,
@@ -227,10 +240,8 @@
     r_recv,
 ):
     comps, _, _, total = u.shape
-    count = total // chunk
+    count = len(spans)
     order = chunk_order(count)
-    sets = chunk_sets(order)
-    set_of = {c: at for at, members in enumerate(sets) for c in members}
     names = ("gx", "gy", "gz")
     place = {name: lax.axis_index(name) for name in names}
     below = {name: place[name] > 0 for name in names}
@@ -244,12 +255,13 @@
     for copy in const_copies:
         copy.start()
     in_copies = {}
-    for c in order:
-        span = pl.ds(c * chunk, chunk)
-        in_copies[c] = pltpu.make_async_copy(
-            u_hbm.at[:, :, :, span], u.at[:, :, :, span], in_sem.at[c]
-        )
-        in_copies[c].start()
+    loads = [[c] for c in order[:2]] + ([sorted(order[2:])] if count > 2 else [])
+    for at, members in enumerate(loads):
+        span = pl.ds(spans[members[0]][0], sum(spans[c][1] for c in members))
+        in_copies[members[0]] = pltpu.make_async_copy(
+            u_hbm.at[:, :, :, span], u.at[:, :, :, span], in_sem.at[at]
+        )
+        in_copies[members[0]].start()
 
     barrier = pltpu.get_barrier_semaphore()
     for name in names:
@@ -262,7 +274,7 @@
                 )
 
     detour = sizes["gx"] == 4
-    relayed = order[: count * 3 // 4] if detour else []
+    relayed = relayed_chunks(spans) if detour else []
     opposite = lax.rem(place["gx"] + 2, 4)
     if detour:
         pl.semaphore_signal(barrier, inc=1, device_id={"gx": opposite}, device_id_type=MESH)
@@ -296,7 +308,7 @@
         metric[:, tile * LANES : (tile + 1) * LANES] = spread * scale[64:72, :]
 
     def span_of(c):
-        return pl.ds(c * chunk, chunk)
+        return pl.ds(*spans[c])
 
     def beside(name, side):
         return {name: place[name] + (1 if side == 0 else -1)}
@@ -309,7 +321,7 @@
     def edge_copy(side, c):
         at = (side, 0, slice(None), span_of(c))
         return remote(
-            x_out.at[at], x_in.at[at], x_send.at[side], edge_recv.at[c], beside("gx", side)
+            x_out.at[at], x_in.at[at], x_send.at[0], edge_recv.at[c], beside("gx", side)
         )
 
     def bulk_copy(side, c):
@@ -317,26 +329,26 @@
         return remote(
             x_out.at[at],
             x_in.at[at],
-            x_send.at[side],
-            bulk_recv.at[set_of[c]],
+            x_send.at[0],
+            bulk_recv.at[c],
             beside("gx", side),
         )
 
     def y_edge_copy(side, c):
         at = (side, 0, slice(None), span_of(c))
         return remote(
-            y_out.at[at], y_in.at[at], y_send.at[side], y_recv.at[set_of[c]], beside("gy", side)
+            y_out.at[at], y_in.at[at], y_send.at[0], y_recv.at[c], beside("gy", side)
         )
 
     def y_bulk_copy(side, c):
         at = (side, slice(1, None), slice(None), span_of(c))
         return remote(
-            y_out.at[at], y_in.at[at], y_send.at[side], y_recv.at[set_of[c]], beside("gy", side)
+            y_out.at[at], y_in.at[at], y_send.at[0], y_recv.at[c], beside("gy", side)
         )
 
     def z_copy(side):
         return remote(
-            z_out.at[side], z_in.at[side], z_send.at[side], z_recv.at[side], beside("gz", side)
+            z_out.at[side], z_in.at[side], z_send.at[0], z_recv.at[0], beside("gz", side)
         )
 
     def middle(side):
@@ -349,7 +361,7 @@
         return remote(
             x_out.at[side, 1:, :, span_of(c)],
             relay.at[:, :, span_of(c)],
-            x_send.at[side],
+            x_send.at[0],
             r_recv.at[relayed.index(c)],
             {"gx": by_way_of(side)},
         )
@@ -359,7 +371,7 @@
             relay.at[:, :, span_of(c)],
             x_in.at[side, 1:, :, span_of(c)],
             r_send.at[0],
-            bulk_recv.at[set_of[c]],
+            bulk_recv.at[c],
             {"gx": 2 - side},
         )
 
@@ -393,17 +405,24 @@
                 hop_copy(side, c).wait_recv()
                 onward_copy(side, c).start()
 
-    def send_bulk(c):
+    def straight(side):
+        if detour:
+            return jnp.logical_and(target("gx", side), jnp.logical_not(middle(side)))
+        return target("gx", side)
+
+    def send_outer(c):
+        for side in range(2):
+            when_do(straight(side), lambda: bulk_copy(side, c).start())
+
+    def send_inner(c):
         for side in range(2):
             if c in relayed:
-                straight = jnp.logical_and(target("gx", side), jnp.logical_not(middle(side)))
-                when_do(straight, lambda: bulk_copy(side, c).start())
                 when_do(middle(side), lambda: hop_copy(side, c).start())
-            else:
-                when_do(target("gx", side), lambda: bulk_copy(side, c).start())
+            elif detour:
+                when_do(middle(side), lambda: bulk_copy(side, c).start())
 
     def y_edges(c):
-        lanes = slice(c * chunk, (c + 1) * chunk)
+        lanes = slice(spans[c][0], sum(spans[c]))
         landed("gx", x_in.at[:, 0, :, span_of(c)], edge_recv.at[c])
         low, high = x_in[0, 0, :, lanes], pltpu.roll(x_in[1, 0, :, lanes], 7, 0)
         for side in range(2):
@@ -421,11 +440,13 @@
     greeted = greeted + (1 if detour else 0)
     waiting, edging = list(relayed), list(order)
     for at, c in enumerate(order):
-        in_copies[c].wait()
-        for start in range(c * chunk, (c + 1) * chunk, STEP):
-            lanes = slice(start, start + STEP)
+        if c in in_copies:
+            in_copies[c].wait()
+        step = spans[c][1]
+        for start in (spans[c][0],):
+            lanes = slice(start, start + step)
             g00, g11, g22, g01, g02, g12 = [metric[k : k + 1, lanes] for k in range(6)]
-            pairs = [split(u[comp, :, :, lanes].reshape(64, STEP)) for comp in range(comps)]
+            pairs = [split(u[comp, :, :, lanes].reshape(64, step)) for comp in range(comps)]
             planes = [
                 product(forward_xy, jnp.concatenate([high, low, high, low], axis=0))
                 for high, low in pairs
@@ -443,13 +464,13 @@
                     product(back_xy, jnp.concatenate([x_high, y_high, x_low, y_low], axis=0))
                 )
             backs_z = along_lanes(z_pairs, back_z)
-            weight = jnp.concatenate([scale[0:64, :]] * (STEP // LANES), axis=1)
+            weight = jnp.concatenate([scale[0:64, :]] * (step // LANES), axis=1)
             ends = ([], [])
             sides = ([], [])
             for comp in range(comps):
                 twice = sums[comp]
                 terms = twice[:64] + twice[64:] + weight * backs_z[comp]
-                terms = terms.reshape(8, 8, STEP)
+                terms = terms.reshape(8, 8, step)
                 local[comp, :, :, lanes] = terms
                 for side, plane in enumerate(y_planes([terms[n] for n in range(8)])):
                     sides[side].append(plane)
@@ -462,20 +483,24 @@
         if at == 0:
             pl.semaphore_wait(barrier, greeted)
         for side in range(2):
-            when_do(target("gx", side), lambda: edge_copy(side, c).start())
+            when_do(straight(side), lambda: edge_copy(side, c).start())
+        for side in range(2):
+            if detour:
+                when_do(middle(side), lambda: edge_copy(side, c).start())
             when_do(target("gy", side), lambda: y_bulk_copy(side, c).start())
-        if at >= BEHIND:
-            send_bulk(order[at - BEHIND])
-        if at >= LAG and edging:
-            y_edges(edging.pop(0))
-        if at >= LAG + 1 and waiting:
-            forward(waiting.pop(0))
-    for c in order[count - min(BEHIND, count) :]:
-        send_bulk(c)
+        if c in relayed:
+            send_inner(c)
+        if 0 <= at - BEHIND < EARLY_BULK:
+            send_outer(order[at - BEHIND])
+    for c in order[min(EARLY_BULK, max(count - BEHIND, 0)) :]:
+        send_outer(c)
+    for c in order:
+        if c not in relayed:
+            send_inner(c)
     while waiting or edging:
         if edging:
             y_edges(edging.pop(0))
-        if waiting:
+        if waiting and count - len(edging) >= EDGES_FIRST:
             forward(waiting.pop(0))
 
     def xy_sum(comp, n, lanes):
@@ -491,11 +516,9 @@
         where = row_index(value.shape)
         return value + jnp.where(where == 0, rows[0], jnp.where(where == 7, rows[1], 0.0))
 
-    def arrived(at):
-        members = sets[at]
-        span = pl.ds(members[0] * chunk, len(members) * chunk)
-        landed("gx", x_in.at[:, 1:, :, span], bulk_recv.at[at])
-        landed("gy", y_in.at[:, :, :, span], y_recv.at[at])
+    def arrived(c):
+        landed("gx", x_in.at[:, 1:, :, span_of(c)], bulk_recv.at[c])
+        landed("gy", y_in.at[:, :, :, span_of(c)], y_recv.at[c])
 
     def finish(first, last):
         for comp in range(comps):
@@ -512,21 +535,35 @@
                 extra = jnp.where(position == 7, after, jnp.where(position == 0, before, 0.0))
                 out[comp, n, :, first:last] = value[:, LANES:-LANES] + extra
 
-    def sent(out_ref, in_ref, send, side):
-        remote(out_ref.at[side], in_ref.at[side], send.at[side], send.at[side], beside("gz", 0)).wait_send()
+    def sent(name, ref, send):
+        def wait(part):
+            remote(part, part, send, send, beside(name, 0)).wait_send()
+
+        if sizes[name] == 2:
+            wait(ref.at[0])
+        elif sizes[name] > 2:
+            both = jnp.logical_and(below[name], above[name])
+            when_do(both, lambda: wait(ref))
+            when_do(jnp.logical_not(both), lambda: wait(ref.at[0]))
 
     def onward_sent():
-        part = relay.at[:, :, pl.ds(0, len(relayed) * chunk)]
+        part = relay.at[:, :, pl.ds(0, sum(spans[c][1] for c in relayed))]
         remote(part, part, r_send.at[0], r_send.at[0], beside("gz", 0)).wait_send()
+
+    def finish_outer():
+        landed("gz", z_in, z_recv.at[0])
+        for t in sorted(outer):
+            finish(t * LANES, (t + 1) * LANES)
 
     tiles = total // LANES
     outer = {0, tiles - 1}
     todo, here = set(range(tiles)) - outer, set()
     ends_here = False
-    for at, members in enumerate(sets):
-        arrived(at)
-        for c in members:
-            here |= set(range(c * chunk // LANES, (c + 1) * chunk // LANES))
+    for at, c in enumerate(order):
+        if at == count - 1 - OUTER_EARLY and at >= 2:
+            finish_outer()
+        arrived(c)
+        here |= set(range(spans[c][0] // LANES, sum(spans[c]) // LANES))
         if outer <= here and not ends_here:
             ends_here = True
             for side in range(2):
@@ -542,24 +579,20 @@
             while ready and ready[0] == last + 1:
                 last = ready.pop(0)
             finish(first * LANES, (last + 1) * LANES)
-    for side in range(2):
-        when_do(source("gz", side), lambda: z_copy(side).wait_recv())
-    for t in sorted(outer):
-        finish(t * LANES, (t + 1) * LANES)
-
-    for side in range(2):
-        when_do(target("gx", side), lambda: sent(x_out, x_in, x_send, side))
-        when_do(target("gy", side), lambda: sent(y_out, y_in, y_send, side))
-        when_do(target("gz", side), lambda: z_copy(side).wait_send())
+    if count - 1 - OUTER_EARLY not in range(2, count):
+        finish_outer()
+
+    sent("gx", x_out, x_send.at[0])
+    sent("gy", y_out, y_send.at[0])
+    sent("gz", z_out, z_send.at[0])
     if relayed:
         when_do(jnp.logical_or(place["gx"] == 0, place["gx"] == 3), onward_sent)
 
 
 def local_part(sizes, nodal_scalar_values, geometry):
     comps, _, _, total = nodal_scalar_values.shape
-    chunk = min(STEP, total)
-    count = total // chunk
-    sets = len(chunk_sets(chunk_order(count)))
+    spans = chunk_spans(total)
+    count = len(spans)
     matrices, scales = tables()
     f32 = jnp.float32
     dma = pltpu.SemaphoreType.DMA
@@ -567,7 +600,7 @@
     plane = pltpu.VMEM((2, comps, 8, total), f32)
     column = pltpu.VMEM((2, comps, 8, 8, LANES), f32)
     return pl.pallas_call(
-        functools.partial(kernel, sizes, chunk),
+        functools.partial(kernel, sizes, spans),
         out_shape=pltpu.VMEM(nodal_scalar_values.shape, f32),
         in_specs=[any_space] * 4,
         out_specs=pl.BlockSpec(memory_space=pltpu.VMEM),
@@ -585,17 +618,17 @@
             column,
             column,
             pltpu.VMEM((comps - 1, 8, total), f32),
-            dma((count,)),
+            dma((min(count, 3),)),
             dma((3,)),
-            dma((2,)),
-            dma((2,)),
-            dma((2,)),
+            dma((1,)),
+            dma((1,)),
+            dma((1,)),
             dma((1,)),
             dma((count,)),
-            dma((sets,)),
-            dma((sets,)),
-            dma((2,)),
-            dma((max(count * 3 // 4, 1),)),
+            dma((count,)),
+            dma((count,)),
+            dma((1,)),
+            dma((max(len(relayed_chunks(spans)), 1),)),
         ],
         compiler_params=pltpu.CompilerParams(collective_id=0, has_side_effects=True),
         name="poisson",

time: 16 us -> 15 us (0.938)
  Pallas kernels: 14.7 us -> 13.7 us
    pallas_call x1, Pallas kernels: 14.7 us -> 13.7 us  [local_part(): pl.pallas_call(functools.partial(kernel, sizes, spans), out_shape=pltpu.V...]
where the time goes in v3:
time: 15 us; the launch traced here: 14.9 us
  Pallas kernels  13.7 us (91%)
  local copies, waits for them, and re-layouts  1.15 us (8%)
    pallas_call x1, Pallas kernels, local_part(): pl.pallas_call(functools.partial(kernel, sizes, spans), out_shape=pltpu.V...  13.7 us
    unnamed x1, local copies, waits for them, and re-layouts  1.15 us

profile of v3, /device:TPU:0, one launch (start us, length us, event | category | flops | bytes accessed | tf_op | source)
XLA Modules:
  0.0 14.9 jit_solution(15721583175883935045)
XLA Ops:
  0.0 13.7 %poisson.1 = f32[3,8,8,2048]{3,2,1,0:T(8,128)S(1)} custom-call(f32[3,8,8,2048]{3,2,1,0:T(8,128)} %u_hbm.1, f32[6,1,1,256]{3,2,1,0:T(1,128)} %geo_hbm.1, bf16[768,256]{1,0:T(8,128)(2,1)} %constant.4.clone.mat_hbm, f32[72,128]{1,0:T(8,128)} %constant.5.clone.scale_hbm), custom_call_target="tpu_custom_call" | custom-call | tf_op jit(solution)/shard_map/poisson/pallas_call | solution.py:602
  13.7 1.1 %copy.6 = f32[3,8,8,2048]{3,2,1,0:T(8,128)} copy(f32[3,8,8,2048]{3,2,1,0:T(8,128)S(1)} %poisson.1) | data formatting | bytes 3145728

commit v4 on v3

--- a/solution.py
+++ b/solution.py
@@ -25,6 +25,7 @@
 RELAYED = 3
 EDGES_FIRST = 2
 OUTER_EARLY = 0
+INNER = 256
 X_EDGE = 7
 Y_EDGE = (6, 7)
 
@@ -236,6 +237,7 @@
     edge_recv,
     bulk_recv,
     y_recv,
+    y_bulk_recv,
     z_recv,
     r_recv,
 ):
@@ -343,12 +345,12 @@
     def y_bulk_copy(side, c):
         at = (side, slice(1, None), slice(None), span_of(c))
         return remote(
-            y_out.at[at], y_in.at[at], y_send.at[0], y_recv.at[c], beside("gy", side)
+            y_out.at[at], y_in.at[at], y_send.at[0], y_bulk_recv.at[0], beside("gy", side)
         )
 
     def z_copy(side):
         return remote(
-            z_out.at[side], z_in.at[side], z_send.at[0], z_recv.at[0], beside("gz", side)
+            z_out.at[side], z_in.at[side], z_send.at[0], z_recv.at[side], beside("gz", side)
         )
 
     def middle(side):
@@ -518,22 +520,29 @@
 
     def arrived(c):
         landed("gx", x_in.at[:, 1:, :, span_of(c)], bulk_recv.at[c])
-        landed("gy", y_in.at[:, :, :, span_of(c)], y_recv.at[c])
-
-    def finish(first, last):
-        for comp in range(comps):
-            for n in range(8):
-                value = xy_sum(comp, n, slice(max(first - LANES, 0), min(last + LANES, total)))
-                if first == 0:
-                    value = jnp.concatenate([z_in[0, comp, n], value], axis=1)
-                if last == total:
-                    value = jnp.concatenate([value, z_in[1, comp, n]], axis=1)
-                width = value.shape[1]
-                before = pltpu.roll(value, 1, 1)[:, LANES:-LANES]
-                after = pltpu.roll(value, width - 1, 1)[:, LANES:-LANES]
-                position = lax.broadcasted_iota(jnp.int32, before.shape, 1) % 8
-                extra = jnp.where(position == 7, after, jnp.where(position == 0, before, 0.0))
-                out[comp, n, :, first:last] = value[:, LANES:-LANES] + extra
+        landed("gy", y_in.at[:, 0, :, span_of(c)], y_recv.at[c])
+
+    every = [(comp, n) for comp in range(comps) for n in range(8)]
+    inner = [
+        (comp, n)
+        for comp, n in every
+        if n not in (0, 7) and y_seat(0, comp, n)[0] and y_seat(1, comp, n)[0]
+    ]
+    outside = [which for which in every if which not in inner]
+
+    def finish(first, last, planes=every):
+        for comp, n in planes:
+            value = xy_sum(comp, n, slice(max(first - LANES, 0), min(last + LANES, total)))
+            if first == 0:
+                value = jnp.concatenate([z_in[0, comp, n], value], axis=1)
+            if last == total:
+                value = jnp.concatenate([value, z_in[1, comp, n]], axis=1)
+            width = value.shape[1]
+            before = pltpu.roll(value, 1, 1)[:, LANES:-LANES]
+            after = pltpu.roll(value, width - 1, 1)[:, LANES:-LANES]
+            position = lax.broadcasted_iota(jnp.int32, before.shape, 1) % 8
+            extra = jnp.where(position == 7, after, jnp.where(position == 0, before, 0.0))
+            out[comp, n, :, first:last] = value[:, LANES:-LANES] + extra
 
     def sent(name, ref, send):
         def wait(part):
@@ -551,14 +560,21 @@
         remote(part, part, r_send.at[0], r_send.at[0], beside("gz", 0)).wait_send()
 
     def finish_outer():
-        landed("gz", z_in, z_recv.at[0])
-        for t in sorted(outer):
-            finish(t * LANES, (t + 1) * LANES)
+        when_do(above["gz"], lambda: z_copy(1).wait_recv())
+        finish(total - LANES, total)
+        when_do(jnp.logical_not(below["gz"]), lambda: finish(0, LANES))
+
+    def finish_first():
+        z_copy(0).wait_recv()
+        finish(0, LANES)
 
     tiles = total // LANES
     outer = {0, tiles - 1}
     todo, here = set(range(tiles)) - outer, set()
     ends_here = False
+    landed("gy", y_in.at[:, 1:], y_bulk_recv.at[0])
+    for first in range(LANES, total - LANES, INNER):
+        finish(first, min(first + INNER, total - LANES), inner)
     for at, c in enumerate(order):
         if at == count - 1 - OUTER_EARLY and at >= 2:
             finish_outer()
@@ -578,9 +594,11 @@
             first = last = ready.pop(0)
             while ready and ready[0] == last + 1:
                 last = ready.pop(0)
-            finish(first * LANES, (last + 1) * LANES)
+            finish(first * LANES, (last + 1) * LANES, outside)
     if count - 1 - OUTER_EARLY not in range(2, count):
         finish_outer()
+
+    when_do(below["gz"], finish_first)
 
     sent("gx", x_out, x_send.at[0])
     sent("gy", y_out, y_send.at[0])
@@ -628,6 +646,7 @@
             dma((count,)),
             dma((count,)),
             dma((1,)),
+            dma((2,)),
             dma((max(len(relayed_chunks(spans)), 1),)),
         ],
         compiler_params=pltpu.CompilerParams(collective_id=0, has_side_effects=True),

time: 15 us -> 14.8 us (0.987)
  Pallas kernels: 13.7 us -> 13.5 us
    pallas_call x1, Pallas kernels: 13.7 us -> 13.5 us  [local_part(): pl.pallas_call(functools.partial(kernel, sizes, spans), out_shape=pltpu.V...]
where the time goes in v4:
time: 14.8 us; the launch traced here: 14.7 us
  Pallas kernels  13.5 us (91%)
  local copies, waits for them, and re-layouts  1.15 us (8%)
    pallas_call x1, Pallas kernels, local_part(): pl.pallas_call(functools.partial(kernel, sizes, spans), out_shape=pltpu.V...  13.5 us
    unnamed x1, local copies, waits for them, and re-layouts  1.15 us

profile of v4, /device:TPU:0, one launch (start us, length us, event | category | flops | bytes accessed | tf_op | source)
XLA Modules:
  0.0 14.7 jit_solution(13608340700095612723)
XLA Ops:
  0.0 13.5 %poisson.1 = f32[3,8,8,2048]{3,2,1,0:T(8,128)S(1)} custom-call(f32[3,8,8,2048]{3,2,1,0:T(8,128)} %u_hbm.1, f32[6,1,1,256]{3,2,1,0:T(1,128)} %geo_hbm.1, bf16[768,256]{1,0:T(8,128)(2,1)} %constant.4.clone.mat_hbm, f32[72,128]{1,0:T(8,128)} %constant.5.clone.scale_hbm), custom_call_target="tpu_custom_call" | custom-call | tf_op jit(solution)/shard_map/poisson/pallas_call | solution.py:620
  13.5 1.1 %copy.6 = f32[3,8,8,2048]{3,2,1,0:T(8,128)} copy(f32[3,8,8,2048]{3,2,1,0:T(8,128)S(1)} %poisson.1) | data formatting | bytes 3145728

commit v5 on v4

--- a/solution.py
+++ b/solution.py
@@ -230,10 +230,6 @@
     relay,
     in_sem,
     const_sem,
-    x_send,
-    y_send,
-    z_send,
-    r_send,
     edge_recv,
     bulk_recv,
     y_recv,
@@ -323,7 +319,7 @@
     def edge_copy(side, c):
         at = (side, 0, slice(None), span_of(c))
         return remote(
-            x_out.at[at], x_in.at[at], x_send.at[0], edge_recv.at[c], beside("gx", side)
+            x_out.at[at], x_in.at[at], const_sem.at[0], edge_recv.at[c], beside("gx", side)
         )
 
     def bulk_copy(side, c):
@@ -331,7 +327,7 @@
         return remote(
             x_out.at[at],
             x_in.at[at],
-            x_send.at[0],
+            const_sem.at[0],
             bulk_recv.at[c],
             beside("gx", side),
         )
@@ -339,18 +335,18 @@
     def y_edge_copy(side, c):
         at = (side, 0, slice(None), span_of(c))
         return remote(
-            y_out.at[at], y_in.at[at], y_send.at[0], y_recv.at[c], beside("gy", side)
+            y_out.at[at], y_in.at[at], const_sem.at[1], y_recv.at[c], beside("gy", side)
         )
 
     def y_bulk_copy(side, c):
         at = (side, slice(1, None), slice(None), span_of(c))
         return remote(
-            y_out.at[at], y_in.at[at], y_send.at[0], y_bulk_recv.at[0], beside("gy", side)
+            y_out.at[at], y_in.at[at], const_sem.at[1], y_bulk_recv.at[0], beside("gy", side)
         )
 
     def z_copy(side):
         return remote(
-            z_out.at[side], z_in.at[side], z_send.at[0], z_recv.at[side], beside("gz", side)
+            z_out.at[side], z_in.at[side], const_sem.at[2], z_recv.at[side], beside("gz", side)
         )
 
     def middle(side):
@@ -363,7 +359,7 @@
         return remote(
             x_out.at[side, 1:, :, span_of(c)],
             relay.at[:, :, span_of(c)],
-            x_send.at[0],
+            const_sem.at[0],
             r_recv.at[relayed.index(c)],
             {"gx": by_way_of(side)},
         )
@@ -372,7 +368,7 @@
         return remote(
             relay.at[:, :, span_of(c)],
             x_in.at[side, 1:, :, span_of(c)],
-            r_send.at[0],
+            in_sem.at[0],
             bulk_recv.at[c],
             {"gx": 2 - side},
         )
@@ -488,10 +484,14 @@
             when_do(straight(side), lambda: edge_copy(side, c).start())
         for side in range(2):
             if detour:
-                when_do(middle(side), lambda: edge_copy(side, c).start())
+
+                @pl.when(middle(side))
+                def _(side=side):
+                    edge_copy(side, c).start()
+                    if c in relayed:
+                        hop_copy(side, c).start()
+
             when_do(target("gy", side), lambda: y_bulk_copy(side, c).start())
-        if c in relayed:
-            send_inner(c)
         if 0 <= at - BEHIND < EARLY_BULK:
             send_outer(order[at - BEHIND])
     for c in order[min(EARLY_BULK, max(count - BEHIND, 0)) :]:
@@ -557,7 +557,7 @@
 
     def onward_sent():
         part = relay.at[:, :, pl.ds(0, sum(spans[c][1] for c in relayed))]
-        remote(part, part, r_send.at[0], r_send.at[0], beside("gz", 0)).wait_send()
+        remote(part, part, in_sem.at[0], in_sem.at[0], beside("gz", 0)).wait_send()
 
     def finish_outer():
         when_do(above["gz"], lambda: z_copy(1).wait_recv())
@@ -600,9 +600,9 @@
 
     when_do(below["gz"], finish_first)
 
-    sent("gx", x_out, x_send.at[0])
-    sent("gy", y_out, y_send.at[0])
-    sent("gz", z_out, z_send.at[0])
+    sent("gx", x_out, const_sem.at[0])
+    sent("gy", y_out, const_sem.at[1])
+    sent("gz", z_out, const_sem.at[2])
     if relayed:
         when_do(jnp.logical_or(place["gx"] == 0, place["gx"] == 3), onward_sent)
 
@@ -638,10 +638,6 @@
             pltpu.VMEM((comps - 1, 8, total), f32),
             dma((min(count, 3),)),
             dma((3,)),
-            dma((1,)),
-            dma((1,)),
-            dma((1,)),
-            dma((1,)),
             dma((count,)),
             dma((count,)),
             dma((count,)),

time: 14.8 us -> 14.8 us (level)
  no operation moved by 1% of the time
where the time goes in v5:
time: 14.8 us; the launch traced here: 14.6 us
  Pallas kernels  13.5 us (91%)
  local copies, waits for them, and re-layouts  1.15 us (8%)
    pallas_call x1, Pallas kernels, local_part(): pl.pallas_call(functools.partial(kernel, sizes, spans), out_shape=pltpu.V...  13.5 us
    unnamed x1, local copies, waits for them, and re-layouts  1.15 us

profile of v5, /device:TPU:0, one launch (start us, length us, event | category | flops | bytes accessed | tf_op | source)
XLA Modules:
  0.0 14.6 jit_solution(3478394584114935591)
XLA Ops:
  0.0 13.5 %poisson.1 = f32[3,8,8,2048]{3,2,1,0:T(8,128)S(1)} custom-call(f32[3,8,8,2048]{3,2,1,0:T(8,128)} %u_hbm.1, f32[6,1,1,256]{3,2,1,0:T(1,128)} %geo_hbm.1, bf16[768,256]{1,0:T(8,128)(2,1)} %constant.4.clone.mat_hbm, f32[72,128]{1,0:T(8,128)} %constant.5.clone.scale_hbm), custom_call_target="tpu_custom_call" | custom-call | tf_op jit(solution)/shard_map/poisson/pallas_call | solution.py:620
  13.5 1.1 %copy.6 = f32[3,8,8,2048]{3,2,1,0:T(8,128)} copy(f32[3,8,8,2048]{3,2,1,0:T(8,128)S(1)} %poisson.1) | data formatting | bytes 3145728
